TPU v7x, 32 devices: a whole 2x2x4 slice. The times are simulated.
32 devices in a mesh: pair: 4 (over y, x), virt: 8 (over z, core).
Axes of the slice: x: 2, y: 2, z: 4, core: 2. Of those that a mesh axis runs over, the one named last changes fastest.
Arguments:
- density_row_blocks: bfloat16 [160, 128, 2744], P('pair', 'virt'), may hold values from -6 to 6
- vir_left: bfloat16 [128, 2744], P('virt'), may hold values from -0.046875 to 0.046875
- vir_right: bfloat16 [128, 2744], P('virt'), may hold values from -0.109375 to 0.109375
- orb_energy: bfloat16 [128], P('virt'), may hold values from 0.5 to 3
- state_energy: float32 [8], replicated, may hold values from -1 to -0.1
- bra_ket_states: int32 [160, 2], P('pair'), may hold values from 0 to 7
- row_block_starts: int32 [160], P('pair'), may hold values from 0 to 2616
Outputs:
- slot_couplings: float32 [160], P('pair')
- heff: float32 [8, 8], replicated
All inputs are finite; a program needn't handle non-finite values.
Results may differ from a plain program's by a relative error of at most 0.0003.
Values may be sent and summed in bfloat16 or wider, within the bound.
No kernel may reach another device: no remote copies, remote signals or barrier semaphores. Data moves between devices by JAX's collectives and lax.ppermute only.
A program may use at most 64 MiB of HBM per device.

v0:
```python
import jax
import jax.numpy as jnp
from jax import lax
from jax.sharding import PartitionSpec as P


def local(
    density_row_blocks,
    vir_left,
    vir_right,
    orb_energy,
    state_energy,
    bra_ket_states,
    row_block_starts,
):
    slots, rows, ntrip = density_row_blocks.shape
    nstate = state_energy.shape[0]
    virt_index = lax.axis_index("virt")
    positions = (
        row_block_starts[:, None] + virt_index * rows + jnp.arange(rows, dtype=jnp.int32)[None, :]
    )
    positions = positions.reshape(slots * rows)
    flat_rdm = density_row_blocks.reshape(slots * rows, ntrip)
    states = jnp.arange(nstate, dtype=jnp.int32)
    first = (bra_ket_states[:, 0:1] == states[None, :]).astype(jnp.float32)
    second = (bra_ket_states[:, 1:2] == states[None, :]).astype(jnp.float32)
    shift = jnp.dot(first + second, state_energy, precision=lax.Precision.HIGHEST)
    columns = jnp.take(lax.all_gather(vir_left, "virt", axis=0, tiled=True), positions, axis=1)
    right_piece = lax.all_gather(vir_right, "virt", axis=0, tiled=True)
    count = right_piece.shape[0]
    contracted = lax.dot_general(
        right_piece, flat_rdm, (((1,), (1,)), ((), ())), preferred_element_type=jnp.float32
    )
    inverse = 1.0 / (
        lax.all_gather(orb_energy, "virt", axis=0, tiled=True).astype(jnp.float32)[:, None]
        - shift[None, :]
    )
    product = columns.astype(jnp.float32).reshape(count, slots, rows) * contracted.reshape(
        count, slots, rows
    )
    partial_sums = jnp.sum(jnp.sum(product, axis=2) * inverse, axis=0)
    couplings = lax.psum(partial_sums, "virt")
    local_sum = jnp.dot(first.T, couplings[:, None] * second, precision=lax.Precision.HIGHEST)
    collected = lax.all_gather(local_sum[None], "pair", axis=0, tiled=True)
    coupling_sum = jnp.sum(collected, axis=0)
    heff = jnp.diag(state_energy) + 0.5 * (coupling_sum + coupling_sum.T)
    return (couplings, heff)


def solution(mesh):
    placed = (
        P("pair", "virt", None),
        P("virt", None),
        P("virt", None),
        P("virt"),
        P(),
        P("pair", None),
        P("pair"),
    )
    return jax.shard_map(
        local, mesh=mesh, in_specs=placed, out_specs=(P("pair"), P()), check_vma=False
    )
```

profile of v0, /device:TPU:0, one launch (start us, length us, event | category | flops | bytes accessed | tf_op | source)
XLA Modules:
  0.0 82.9 jit_solution(17060475857912333870)
XLA Ops:
  0.6 0.0 copy-start
  0.6 0.7 broadcast_add_fusion
  1.3 0.1 copy.22
  1.4 0.1 add.74
  1.5 17.2 %all_gather.12 = bf16[128,2744]{1,0:T(8,128)(2,1)S(1)} all-gather(bf16[16,2744]{1,0:T(8,128)(2,1)} %param.8), channel_id=1, replica_groups=mesh['pair'=4,'virt'=8] {'virt'}, dimensions={0}, use_global_device_ids=true | all-gather | bytes 790272 | tf_op jit(solution)/shard_map/all_gather | solution.py:28
  18.8 0.4 copy.23
  19.1 2.0 %gather_fusion = bf16[640,128]{1,0:T(8,128)(2,1)S(1)} fusion(bf16[128,2744]{0,1:T(8,128)(2,1)S(1)} %copy.23, s32[1024]{0:T(1024)S(1)} %pad_clamp_fusion), kind=kCustom, calls=%fused_computation | custom fusion | bytes 330240 | tf_op jit(solution)/shard_map/jit(_take)/gather | solution.py:28
  21.1 0.0 copy-start.1
  21.2 0.0 copy-start.2
  21.2 0.0 copy-start.4
  21.2 0.0 copy-start.3
  21.2 0.0 copy-done
  21.2 15.5 %all_gather.13 = bf16[128,2744]{1,0:T(8,128)(2,1)S(1)} all-gather(bf16[16,2744]{1,0:T(8,128)(2,1)S(1)} %copy-done), channel_id=1, replica_groups=mesh['pair'=4,'virt'=8] {'virt'}, dimensions={0}, use_global_device_ids=true | all-gather | bytes 790272 | tf_op jit(solution)/shard_map/all_gather | solution.py:29
  36.7 3.8 %fusion.5 = f32[128,40]{0,1:T(8,128)S(1)} fusion(bf16[40,16,2744]{2,1,0:T(8,128)(2,1)} %param.7, bf16[128,2744]{1,0:T(8,128)(2,1)S(1)} %all_gather.13, bf16[128,40,16]{0,2,1:T(8,128)(2,1)S(1)} %bitcast.24, pred[40,16]{0,1:T(8,128)(4,1)S(1)} %compare_and_fusion), kind=kOutput, calls=%fused_computation.4 | convolution fusion | flops 449899520 | bytes 4399744 | tf_op jit(solution)/shard_map/dot_general | solution.py:31
  40.5 0.0 copy-done.1
  40.5 0.0 copy-done.2
  40.5 0.2 convolution_bitcast_fusion
  40.7 0.0 copy-done.4
  40.7 0.6 dynamic-slice
  42.0 0.0 copy-done.3
  42.0 0.2 dynamic-update-slice
  42.2 17.7 %all-reduce = bf16[128]{0:T(256)(128)(2,1)S(1)} all-reduce(bf16[128]{0:T(256)(128)(2,1)S(1)} %dynamic-update-slice), channel_id=1, replica_groups=mesh['pair'=4,'virt'=8] {'virt'}, use_global_device_ids=true, to_apply=%add | all-reduce | flops 128 | bytes 512
  60.0 0.2 multiply_reduce_fusion
  60.1 13.6 %psum.7 = f32[40]{0:T(128)S(1)} all-reduce(f32[40]{0:T(128)S(1)} %multiply_reduce_fusion), channel_id=1, replica_groups=mesh['pair'=4,'virt'=8] {'virt'}, use_global_device_ids=true, to_apply=%region_2.3 | all-reduce | flops 40 | bytes 320 | tf_op jit(solution)/shard_map/psum | solution.py:42
  73.7 0.0 copy-start.5
  73.7 0.3 fusion.9
  74.0 8.2 %all-gather = f32[32,8]{1,0:T(8,128)S(1)} all-gather(f32[8,8]{1,0:T(8,128)S(1)} %fusion.9), channel_id=2, replica_groups=mesh['pair'=4,'virt'=8] {'pair'}, dimensions={0}, use_global_device_ids=true | all-gather | bytes 1280 | tf_op jit(solution)/shard_map/all_gather | solution.py:44
  82.2 0.1 copy.26
  82.3 0.7 fusion.21
  82.9 0.0 copy-done.5
  (8 shorter events, 0.1 us)
Async XLA Ops:
  0.6 20.6 %copy-start = (bf16[16,2744]{1,0:T(8,128)(2,1)S(1)}, bf16[16,2744]{1,0:T(8,128)(2,1)}, u32[]{:S(2)}) copy-start(bf16[16,2744]{1,0:T(8,128)(2,1)} %param.9) | copy-start | bytes 263428
  21.1 19.3 %copy-start.1 = (s32[40,2]{0,1:T(2,128)S(1)}, s32[40,2]{0,1:T(2,128)}, u32[]{:S(2)}) copy-start(s32[40,2]{0,1:T(2,128)} %param.12) | copy-start | bytes 964
  21.2 19.3 %copy-start.2 = (f32[8]{0:T(128)S(1)}, f32[8]{0:T(128)}, u32[]{:S(2)}) copy-start(f32[8]{0:T(128)} %param.11) | copy-start | bytes 100
  21.2 19.5 %copy-start.4 = (u32[32]{0:T(128)S(1)}, u32[32]{0:T(128)}, u32[]{:S(2)}) copy-start(u32[32]{0:T(128)} %constant.33) | copy-start | bytes 388
  21.2 20.8 %copy-start.3 = (bf16[16]{0:T(256)(128)(2,1)S(1)}, bf16[16]{0:T(256)(128)(2,1)}, u32[]{:S(2)}) copy-start(bf16[16]{0:T(256)(128)(2,1)} %param.10) | copy-start | bytes 100
  73.7 9.2 %copy-start.5 = (f32[40]{0:T(128)}, f32[40]{0:T(128)S(1)}, u32[]{:S(2)}) copy-start(f32[40]{0:T(128)S(1)} %psum.7) | copy-start | bytes 484
where the time goes:
time: 83.2 us; the launch traced here: 82.9 us
  blocking collectives  72.2 us (87%)
  matrix products  4.26 us (5%)
  local copies, waits for them, and re-layouts  3.48 us (4%)
  other arithmetic  1.59 us (2%)
  between operations  1.41 us (2%)
    unnamed x1, blocking collectives  17.7 us
    all_gather x1, blocking collectives, local(): lax.all_gather(vir_left, 'virt', axis=0, tiled=True)  17.2 us
    all_gather x1, blocking collectives, local(): right_piece = lax.all_gather(vir_right, 'virt', axis=0, tiled=True)  15.5 us
    psum x1, blocking collectives, local(): couplings = lax.psum(partial_sums, 'virt')  13.6 us
    all_gather x1, blocking collectives, local(): collected = lax.all_gather(local_sum[None], 'pair', axis=0, tiled=True)  8.18 us
    dot_general x1, matrix products, local(): lax.dot_general(right_piece, flat_rdm, (((1,), (1,)), ((), ())), preferre...  3.8 us
    gather x1, local copies, waits for them, and re-layouts, local(): jnp.take(lax.all_gather(vir_left, 'virt', axis=0, tiled=True), positions,...  1.99 us

commit v1 on v0

v1 whole, which is shorter than its diff:
```python
import functools

import jax
import jax.numpy as jnp
from jax import lax
from jax.experimental import pallas as pl
from jax.experimental.pallas import tpu as pltpu
from jax.sharding import Mesh
from jax.sharding import PartitionSpec as P

LANES = 128


def rotate(x, axis, size, step):
    return lax.ppermute(x, axis, [(i, (i + step) % size) for i in range(size)])


def flip(x, axis, size, bits):
    return lax.ppermute(x, axis, [(i, i ^ bits) for i in range(size)])


def all_sum2(x, axis, size):
    bits = 1
    while bits < size:
        x = x + flip(x, axis, size, bits)
        bits *= 2
    return x


def all_sum4(x, axis, size):
    bits = 1
    while bits * 4 <= size:
        one, two, three = (flip(x, axis, size, bits * k) for k in (1, 2, 3))
        x = (x + one) + (two + three)
        bits *= 4
    while bits < size:
        x = x + flip(x, axis, size, bits)
        bits *= 2
    return x


def window_kernel(where_ref, starts_ref, left_ref, out_ref, wide_ref, *, nz, ncore, slots, rows):
    own, ntrip = left_ref.shape
    per = LANES // rows
    wide_ref[:, :ntrip] = left_ref[...].astype(jnp.float32)
    lane_group = lax.broadcasted_iota(jnp.int32, (own, LANES), 1) // rows
    my_z = where_ref[0]
    my_core = where_ref[1]

    def one(block, carry):
        step = block // ncore
        dest_z = lax.rem(my_z + step, nz)
        dest_core = lax.rem(my_core + lax.rem(block, ncore), ncore)
        shift = (dest_z * ncore + dest_core) * rows
        for group in range(-(-slots // per)):
            acc = jnp.zeros((own, LANES), jnp.float32)
            for j in range(min(per, slots - group * per)):
                at = starts_ref[group * per + j] + shift
                base = pl.multiple_of((at // LANES) * LANES, LANES)
                pair = wide_ref[:, pl.ds(base, 2 * LANES)]
                turn = lax.rem(j * rows - (at - base) + 2 * LANES, 2 * LANES)
                acc = jnp.where(lane_group == j, pltpu.roll(pair, turn, 1)[:, :LANES], acc)
            out_ref[block, :, group * LANES : (group + 1) * LANES] = acc.astype(out_ref.dtype)
        return carry

    lax.fori_loop(0, nz * ncore, one, 0)


def windows(left, starts, where, nz, ncore, rows):
    own, ntrip = left.shape
    slots = starts.shape[0]
    per = LANES // rows
    wide = (ntrip // LANES + 2) * LANES
    width = -(-slots // per) * LANES
    return pl.pallas_call(
        functools.partial(
            window_kernel, nz=nz, ncore=ncore, slots=slots, rows=rows
        ),
        out_shape=jax.ShapeDtypeStruct((nz * ncore, own, width), left.dtype),
        in_specs=[
            pl.BlockSpec(memory_space=pltpu.SMEM),
            pl.BlockSpec(memory_space=pltpu.SMEM),
            pl.BlockSpec(memory_space=pltpu.VMEM),
        ],
        out_specs=pl.BlockSpec(memory_space=pltpu.VMEM),
        scratch_shapes=[pltpu.VMEM((own, wide), jnp.float32)],
        name="windows",
    )(where, starts, left)


def couple_kernel(*refs, parts, ntrip, block):
    left_refs, right_refs = refs[:parts], refs[parts : 2 * parts]
    shift_ref, rdm_ref, out_ref, right_ref, energy_ref = refs[2 * parts :]
    at = 0
    for piece in right_refs:
        size = piece.shape[0]
        right_ref[at : at + size, :] = piece[:, :ntrip]
        energy_ref[at : at + size, :] = piece[:, ntrip : ntrip + 1].astype(jnp.float32)
        at += size
    total = rdm_ref.shape[0]
    for begin in range(0, total, block):
        cut = slice(begin, min(begin + block, total))
        contracted = lax.dot_general(
            right_ref[...],
            rdm_ref[cut, :],
            (((1,), (1,)), ((), ())),
            preferred_element_type=jnp.float32,
        )
        left = jnp.concatenate([piece[:, cut].astype(jnp.float32) for piece in left_refs], axis=0)
        inverse = 1.0 / (energy_ref[...] - shift_ref[:, cut])
        out_ref[:, cut] = jnp.sum(left * contracted * inverse, axis=0, keepdims=True)


def couple(lefts, rights, shift, rdm, block):
    total, ntrip = rdm.shape
    count = sum(piece.shape[0] for piece in rights)
    vmem = pl.BlockSpec(memory_space=pltpu.VMEM)
    return pl.pallas_call(
        functools.partial(couple_kernel, parts=len(rights), ntrip=ntrip, block=block),
        out_shape=jax.ShapeDtypeStruct((1, total), jnp.float32),
        in_specs=[vmem] * (2 * len(rights) + 2),
        out_specs=vmem,
        scratch_shapes=[
            pltpu.VMEM((count, ntrip), rdm.dtype),
            pltpu.VMEM((count, 1), jnp.float32),
        ],
        name="couple",
    )(*lefts, *rights, shift, rdm)


def local(
    density_row_blocks,
    vir_left,
    vir_right,
    orb_energy,
    state_energy,
    bra_ket_states,
    row_block_starts,
    *,
    npair,
    nz,
    ncore,
):
    slots, rows, ntrip = density_row_blocks.shape
    own = vir_right.shape[0]
    nstate = state_energy.shape[0]

    packed = jnp.concatenate([vir_right, orb_energy[:, None]], axis=1)
    right = [packed] + [rotate(packed, "z", nz, k) for k in range(1, nz)]

    where = jnp.stack([lax.axis_index("z"), lax.axis_index("core")]).astype(jnp.int32)
    cut = windows(vir_left, row_block_starts, where, nz, ncore, rows)
    cut = cut.reshape(nz, ncore, own, cut.shape[-1])
    left = [cut[0]] + [rotate(cut[k], "z", nz, k) for k in range(1, nz)]

    rights, lefts = list(right), [piece[0] for piece in left]
    if ncore > 1:
        right = jnp.concatenate(right, axis=0)
        left = jnp.stack(left)
        for k in range(1, ncore):
            rights.append(rotate(right, "core", ncore, k))
            lefts.append(rotate(left[:, k].reshape(nz * own, -1), "core", ncore, k))

    states = jnp.arange(nstate, dtype=jnp.int32)
    first = (bra_ket_states[:, 0:1] == states[None, :]).astype(jnp.float32)
    second = (bra_ket_states[:, 1:2] == states[None, :]).astype(jnp.float32)
    shift = jnp.dot(first + second, state_energy, precision=lax.Precision.HIGHEST)
    flat_rdm = density_row_blocks.reshape(slots * rows, ntrip)
    wide_shift = jnp.repeat(shift, rows)[None, :]
    sums = couple(lefts, rights, wide_shift, flat_rdm, 2 * LANES)
    partial_sums = jnp.sum(sums.reshape(slots, rows), axis=1)

    couplings = all_sum2(all_sum2(partial_sums, "core", ncore), "z", nz)
    local_sum = jnp.dot(first.T, couplings[:, None] * second, precision=lax.Precision.HIGHEST)
    coupling_sum = all_sum4(local_sum, "pair", npair)
    heff = jnp.diag(state_energy) + 0.5 * (coupling_sum + coupling_sum.T)
    return (couplings, heff)


def solution(mesh):
    npair, nvirt = mesh.shape["pair"], mesh.shape["virt"]
    ncore = 2 if nvirt % 2 == 0 else 1
    nz = nvirt // ncore
    split = Mesh(mesh.devices.reshape(npair, nz, ncore), ("pair", "z", "core"))
    virt = ("z", "core")
    placed = (
        P("pair", virt, None),
        P(virt, None),
        P(virt, None),
        P(virt),
        P(),
        P("pair", None),
        P("pair"),
    )
    return jax.shard_map(
        functools.partial(local, npair=npair, nz=nz, ncore=ncore),
        mesh=split,
        in_specs=placed,
        out_specs=(P("pair"), P()),
        check_vma=False,
    )
```

time: 83.2 us -> 51.8 us (0.62)
  blocking collectives: 72.2 us -> 0 us
  starting transfers between devices: 0 us -> 16.6 us
  waiting for transfers between devices: 0 us -> 13.2 us
  Pallas kernels: 0 us -> 9.48 us
  local copies, waits for them, and re-layouts: 3.48 us -> 7.16 us
  matrix products: 4.26 us -> 1.11 us
  other arithmetic: 1.59 us -> 3.16 us
    all_gather x3 -> x0, blocking collectives: 40.9 us -> none  [the longest x1 17.2 us: local(): lax.all_gather(vir_left, 'virt', axis=0, tiled=True)]
    unnamed x1 -> x0, blocking collectives: 17.7 us -> none
    ppermute x0 -> x14, starting transfers between devices: none -> 16.6 us  [the longest x8 10.3 us: rotate(): return lax.ppermute(x, axis, [(i, (i + step) % size) for i in range(size)])]
    psum x1 -> x0, blocking collectives: 13.6 us -> none  [local(): couplings = lax.psum(partial_sums, 'virt')]
    ppermute x0 -> x14, waiting for transfers between devices: none -> 13.2 us  [the longest x6 9.53 us: flip(): return lax.ppermute(x, axis, [(i, i ^ bits) for i in range(size)])]
    pallas_call x0 -> x2, Pallas kernels: none -> 9.48 us  [the longest x1 5.25 us: windows(): pl.pallas_call(functools.partial(window_kernel, nz=nz, ncore=ncore, slots...]
    dot_general x1 -> x0, matrix products: 3.8 us -> none  [local(): lax.dot_general(right_piece, flat_rdm, (((1,), (1,)), ((), ())), preferre...]
    squeeze x0 -> x4, local copies, waits for them, and re-layouts: none -> 3.13 us  [local(): rights, lefts = (list(right), [piece[0] for piece in left])]
  transfers between devices with their start and end apart: 0 -> 14, of which waited for: 0 -> 8; matrix products, arithmetic and copies ran while one was open for 0% -> 14% of each run, Pallas kernels for 0% -> 10%
where the time goes in v1:
time: 51.8 us; the launch traced here: 51.4 us
  starting transfers between devices  16.6 us (32%)
  waiting for transfers between devices  13.2 us (25%)
  Pallas kernels  9.48 us (18%)
  local copies, waits for them, and re-layouts  7.16 us (14%)
  other arithmetic  3.16 us (6%)
  matrix products  1.11 us (2%)
  between operations  0.72 us (1%)
    ppermute x8, starting transfers between devices, rotate(): return lax.ppermute(x, axis, [(i, (i + step) % size) for i in range(size)])  10.3 us
    ppermute x6, waiting for transfers between devices, flip(): return lax.ppermute(x, axis, [(i, i ^ bits) for i in range(size)])  9.53 us
    ppermute x6, starting transfers between devices, flip(): return lax.ppermute(x, axis, [(i, i ^ bits) for i in range(size)])  6.29 us
    pallas_call x1, Pallas kernels, windows(): pl.pallas_call(functools.partial(window_kernel, nz=nz, ncore=ncore, slots...  5.25 us
    pallas_call x1, Pallas kernels, couple(): pl.pallas_call(functools.partial(couple_kernel, parts=len(rights), ntrip=...  4.23 us
    ppermute x8, waiting for transfers between devices, rotate(): return lax.ppermute(x, axis, [(i, (i + step) % size) for i in range(size)])  3.63 us
    squeeze x4, local copies, waits for them, and re-layouts, local(): rights, lefts = (list(right), [piece[0] for piece in left])  3.13 us
  transfers between devices with their start and end apart: 14, of which 8 were waited for; matrix products, arithmetic and copies ran while one was open for 14% of the time, Pallas kernels for 10%

profile of v1, /device:TPU:0, one launch (start us, length us, event | category | flops | bytes accessed | tf_op | source)
XLA Modules:
  0.0 51.4 jit_solution(1704804427808614860)
XLA Ops:
  0.6 0.0 copy-start.6
  0.6 0.7 %copy.11 = bf16[16,1]{1,0:T(8,128)(2,1)S(1)} copy(bf16[16,1]{0,1:T(2,128)(2,1)} %bitcast.38) | data formatting | bytes 64 | tf_op jit(solution)/shard_map/broadcast_in_dim | solution.py:148
  1.4 1.0 %pad_maximum_fusion.1.refs_5_ = bf16[16,2745]{1,0:T(8,128)(2,1)S(1)} fusion(bf16[16,1]{1,0:T(8,128)(2,1)S(1)} %copy.11, bf16[16,2744]{1,0:T(8,128)(2,1)} %param.9), kind=kLoop, calls=%fused_computation.2 | loop fusion | flops 175680 | bytes 175680 | tf_op jit(solution)/shard_map/concatenate | solution.py:148
  2.4 3.1 %collective-permute-start.4 = (bf16[16,2745]{1,0:T(8,128)(2,1)S(1)}, bf16[16,2745]{1,0:T(8,128)(2,1)S(1)}, u32[]{:S(2)}, u32[]{:S(2)}) collective-permute-start(bf16[16,2745]{1,0:T(8,128)(2,1)S(1)} %pad_maximum_fusion.1.refs_5_), channel_id=1, source_target_pairs={{0,2},{2,4},{4,6},{6,0},{1,3},{3,5},{5,7},{7,1},{8,10},{10,12},{12... | collective-permute-start | bytes 263528 | tf_op jit(solution)/shard_map/ppermute | solution.py:15
  5.4 2.6 %collective-permute-start.5 = (bf16[16,2745]{1,0:T(8,128)(2,1)S(1)}, bf16[16,2745]{1,0:T(8,128)(2,1)S(1)}, u32[]{:S(2)}, u32[]{:S(2)}) collective-permute-start(bf16[16,2745]{1,0:T(8,128)(2,1)S(1)} %pad_maximum_fusion.1.refs_5_), channel_id=1, source_target_pairs={{0,4},{2,6},{4,0},{6,2},{1,5},{3,7},{5,1},{7,3},{8,12},{10,14},{12... | collective-permute-start | bytes 263528 | tf_op jit(solution)/shard_map/ppermute | solution.py:15
  8.0 0.7 %pad_add_fusion.where_ref = s32[2]{0:T(128)} fusion(s32[1]{0:T(128)} %bitcast.1, s32[1]{0:T(128)} %bitcast), kind=kLoop, calls=%fused_computation.29 | loop fusion | flops 2 | bytes 16 | tf_op jit(solution)/shard_map/stack | solution.py:151
  8.7 5.3 %windows.1 = bf16[8,16,640]{2,1,0:T(8,128)(2,1)} custom-call(s32[2]{0:T(128)} %pad_add_fusion.where_ref, s32[40]{0:T(128)} %starts_ref.1, bf16[16,2744]{1,0:T(8,128)(2,1)} %left_ref.1), custom_call_target="tpu_custom_call" | custom-call | tf_op jit(solution)/shard_map/windows/pallas_call | solution.py:75
  13.9 0.9 %slice_bitcast_fusion = (bf16[1,2,16,640]{3,2,1,0:T(8,128)(2,1)S(1)}, bf16[2,16,640]{2,1,0:T(8,128)(2,1)S(1)}, bf16[2,16,640]{2,1,0:T(8,128)(2,1)S(1)}, bf16[2,16,640]{2,1,0:T(8,128)(2,1)S(1)}) fusion(bf16[8,16,640]{2,1,0:T(8,128)(2,1)} %windows.1), kind=kLoop, calls=%fused_computation.6 | loop fusion | bytes 327680 | tf_op jit(solution)/shard_map/slice | solution.py:154
  14.8 0.1 collective-permute-start
  14.9 1.8 %collective-permute-start.1 = (bf16[2,16,640]{2,1,0:T(8,128)(2,1)S(1)}, bf16[2,16,640]{2,1,0:T(8,128)(2,1)S(1)}, u32[]{:S(2)}, u32[]{:S(2)}) collective-permute-start(bf16[2,16,640]{2,1,0:T(8,128)(2,1)S(1)} %get-tuple-element.4), channel_id=1, source_target_pairs={{0,4},{2,6},{4,0},{6,2},{1,5},{3,7},{5,1},{7,3},{8,12},{10,14},{12... | collective-permute-start | bytes 122888 | tf_op jit(solution)/shard_map/ppermute | solution.py:15
  16.7 1.9 %collective-permute-start.2 = (bf16[2,16,640]{2,1,0:T(8,128)(2,1)S(1)}, bf16[2,16,640]{2,1,0:T(8,128)(2,1)S(1)}, u32[]{:S(2)}, u32[]{:S(2)}) collective-permute-start(bf16[2,16,640]{2,1,0:T(8,128)(2,1)S(1)} %get-tuple-element.3), channel_id=1, source_target_pairs={{0,6},{2,0},{4,2},{6,4},{1,7},{3,1},{5,3},{7,5},{8,14},{10,8},{12,... | collective-permute-start | bytes 122888 | tf_op jit(solution)/shard_map/ppermute | solution.py:15
  18.7 1.3 %slice_bitcast_fusion.4.refs_0_ = bf16[16,640]{1,0:T(8,128)(2,1)} fusion(bf16[8,16,640]{2,1,0:T(8,128)(2,1)} %windows.1), kind=kLoop, calls=%fused_computation.10 | loop fusion | bytes 40960 | tf_op jit(solution)/shard_map/squeeze | solution.py:156
  20.0 0.8 %slice_bitcast_fusion.6 = (s32[40]{0:T(128)S(1)}, s32[40]{0:T(128)S(1)}) fusion(s32[40,2]{0,1:T(2,128)} %param.12), kind=kLoop, calls=%fused_computation.32 | loop fusion | bytes 640 | tf_op jit(solution)/shard_map/eq | solution.py:165
  20.7 0.9 %convolution_bitcast_fusion = f32[40]{0:T(128)S(1)} fusion(s32[40]{0:T(128)S(1)} %get-tuple-element.7, s32[40]{0:T(128)S(1)} %get-tuple-element.6, f32[8]{0:T(128)} %param.11), kind=kOutput, calls=%fused_computation | convolution fusion | flops 5440 | bytes 512 | tf_op jit(solution)/shard_map/dot_general | solution.py:167
  21.6 0.1 broadcast_in_dim.28
  21.7 0.7 %broadcast_in_dim_reshape.3.refs_10_ = f32[1,640]{1,0:T(1,128)} reshape(f32[40,16]{1,0:T(8,128)S(1)} %broadcast_in_dim.28) | data formatting | bytes 5120 | tf_op jit(solution)/shard_map/broadcast_in_dim;reshape | solution.py:169
  22.4 0.0 collective-permute-done
  22.4 0.6 %collective-permute-start.6 = (bf16[16,2745]{1,0:T(8,128)(2,1)S(1)}, bf16[16,2745]{1,0:T(8,128)(2,1)S(1)}, u32[]{:S(2)}, u32[]{:S(2)}) collective-permute-start(bf16[16,2745]{1,0:T(8,128)(2,1)S(1)} %pad_maximum_fusion.1.refs_5_), channel_id=1, source_target_pairs={{0,6},{2,0},{4,2},{6,4},{1,7},{3,1},{5,3},{7,5},{8,14},{10,8},{12,... | collective-permute-start | bytes 263528 | tf_op jit(solution)/shard_map/ppermute | solution.py:15
  23.0 0.1 collective-permute-start.3
  23.1 0.6 %slice_bitcast_fusion.3.refs_1_ = bf16[16,640]{1,0:T(8,128)(2,1)} fusion(bf16[2,16,640]{2,1,0:T(8,128)(2,1)S(1)} %collective-permute-done), kind=kLoop, calls=%fused_computation.9 | loop fusion | bytes 40960 | tf_op jit(solution)/shard_map/squeeze | solution.py:156
  23.7 0.0 collective-permute-done.5.refs_7_
  23.7 3.2 %collective-permute-done.6.refs_8_ = bf16[16,2745]{1,0:T(8,128)(2,1)S(1)} collective-permute-done((bf16[16,2745]{1,0:T(8,128)(2,1)S(1)}, bf16[16,2745]{1,0:T(8,128)(2,1)S(1)}, u32[]{:S(2)}, u32[]{:S(2)}) %collective-permute-start.6) | collective-permute-done | bytes 87872 | tf_op jit(solution)/shard_map/ppermute | solution.py:15
  26.9 0.1 collective-permute-start.7
  27.0 0.6 %slice_bitcast_fusion.2.refs_2_ = bf16[16,640]{1,0:T(8,128)(2,1)} fusion(bf16[2,16,640]{2,1,0:T(8,128)(2,1)S(1)} %collective-permute-done.1), kind=kLoop, calls=%fused_computation.8 | loop fusion | bytes 40960 | tf_op jit(solution)/shard_map/squeeze | solution.py:156
  27.6 0.6 %slice_bitcast_fusion.1.refs_3_ = bf16[16,640]{1,0:T(8,128)(2,1)} fusion(bf16[2,16,640]{2,1,0:T(8,128)(2,1)S(1)} %collective-permute-done.2), kind=kLoop, calls=%fused_computation.7 | loop fusion | bytes 40960 | tf_op jit(solution)/shard_map/squeeze | solution.py:156
  28.2 0.0 collective-permute-done.3.refs_4_
  28.2 0.5 collective-permute-done.7.refs_9_
  28.7 0.2 copy-done.5
  28.9 0.6 %copy-done.1 = bf16[64,2745]{1,0:T(8,128)(2,1)} copy-done((bf16[64,2745]{1,0:T(8,128)(2,1)}, bf16[64,2745]{1,0:T(8,128)(2,1)S(1)}, u32[]{:S(2)}) %copy-start.1) | copy-done | bytes 351384
  29.4 4.2 %couple.1 = f32[1,640]{1,0:T(1,128)} custom-call(bf16[16,640]{1,0:T(8,128)(2,1)} %slice_bitcast_fusion.4.refs_0_, bf16[16,640]{1,0:T(8,128)(2,1)} %slice_bitcast_fusion.3.refs_1_, bf16[16,640]{1,0:T(8,128)(2,1)} %slice_bitcast_fusion.2.refs_2_, bf16[16,640]{1,0:T(8,128)(2,1)} %slice_bitcast_fusion.1.refs_3_, bf16[64,640]{1,0:T(8,128)(2,1)} %copy-done.5, ...), custom_call_target="tpu_custom_call" | custom-call | tf_op jit(solution)/shard_map/couple/pallas_call | solution.py:118
  33.7 0.7 %reduce = f32[640]{0:T(1024)S(1)} reduce(f32[1,640]{1,0:T(1,128)} %couple.1, f32[]{:T(128)} %constant.15), dimensions={0}, to_apply=%pallas_call.7.reduce_sub_computation | reduce | bytes 5124 | tf_op jit(solution)/shard_map/couple/pallas_call | solution.py:118
  34.4 0.1 reshape.24
  34.4 0.1 reduce_sum.9
  34.5 0.2 collective-permute-start.8
  34.7 1.0 %collective-permute-done.8 = f32[40]{0:T(128)S(1)} collective-permute-done((f32[40]{0:T(128)S(1)}, f32[40]{0:T(128)S(1)}, u32[]{:S(2)}, u32[]{:S(2)}) %collective-permute-start.8) | collective-permute-done | bytes 192 | tf_op jit(solution)/shard_map/ppermute | solution.py:19
  35.8 0.6 %collective-permute-start.9 = (f32[40]{0:T(128)S(1)}, f32[40]{0:T(128)S(1)}, u32[]{:S(2)}, u32[]{:S(2)}) collective-permute-start(f32[40]{0:T(128)S(1)} %add.28), channel_id=1, source_target_pairs={{0,2},{2,0},{4,6},{6,4},{1,3},{3,1},{5,7},{7,5},{8,10},{10,8},{12,... | collective-permute-start | bytes 488 | tf_op jit(solution)/shard_map/ppermute | solution.py:19
  36.3 3.0 %collective-permute-done.9 = f32[40]{0:T(128)S(1)} collective-permute-done((f32[40]{0:T(128)S(1)}, f32[40]{0:T(128)S(1)}, u32[]{:S(2)}, u32[]{:S(2)}) %collective-permute-start.9) | collective-permute-done | bytes 192 | tf_op jit(solution)/shard_map/ppermute | solution.py:19
  39.3 2.0 %collective-permute-start.10 = (f32[40]{0:T(128)S(1)}, f32[40]{0:T(128)S(1)}, u32[]{:S(2)}, u32[]{:S(2)}) collective-permute-start(f32[40]{0:T(128)S(1)} %add.29), channel_id=1, source_target_pairs={{0,4},{2,6},{4,0},{6,2},{1,5},{3,7},{5,1},{7,3},{8,12},{10,14},{12... | collective-permute-start | bytes 488 | tf_op jit(solution)/shard_map/ppermute | solution.py:19
  41.4 2.4 %collective-permute-done.10 = f32[40]{0:T(128)S(1)} collective-permute-done((f32[40]{0:T(128)S(1)}, f32[40]{0:T(128)S(1)}, u32[]{:S(2)}, u32[]{:S(2)}) %collective-permute-start.10) | collective-permute-done | bytes 192 | tf_op jit(solution)/shard_map/ppermute | solution.py:19
  43.8 0.3 fusion
  44.1 1.5 %collective-permute-start.12 = (f32[8,8]{1,0:T(8,128)S(1)}, f32[8,8]{1,0:T(8,128)S(1)}, u32[]{:S(2)}, u32[]{:S(2)}) collective-permute-start(f32[8,8]{1,0:T(8,128)S(1)} %fusion), channel_id=1, source_target_pairs={{0,16},{8,24},{16,0},{24,8},{1,17},{9,25},{17,1},{25,9},{2,18},{10... | collective-permute-start | bytes 776 | tf_op jit(solution)/shard_map/ppermute | solution.py:19
  45.6 1.4 %collective-permute-start.13 = (f32[8,8]{1,0:T(8,128)S(1)}, f32[8,8]{1,0:T(8,128)S(1)}, u32[]{:S(2)}, u32[]{:S(2)}) collective-permute-start(f32[8,8]{1,0:T(8,128)S(1)} %fusion), channel_id=1, source_target_pairs={{0,24},{8,16},{16,8},{24,0},{1,25},{9,17},{17,9},{25,1},{2,26},{10... | collective-permute-start | bytes 776 | tf_op jit(solution)/shard_map/ppermute | solution.py:19
  47.0 0.5 %collective-permute-start.11 = (f32[8,8]{1,0:T(8,128)S(1)}, f32[8,8]{1,0:T(8,128)S(1)}, u32[]{:S(2)}, u32[]{:S(2)}) collective-permute-start(f32[8,8]{1,0:T(8,128)S(1)} %fusion), channel_id=1, source_target_pairs={{0,8},{8,0},{16,24},{24,16},{1,9},{9,1},{17,25},{25,17},{2,10},{10... | collective-permute-start | bytes 776 | tf_op jit(solution)/shard_map/ppermute | solution.py:19
  47.6 0.1 collective-permute-done.12
  47.7 2.4 %collective-permute-done.13 = f32[8,8]{1,0:T(8,128)S(1)} collective-permute-done((f32[8,8]{1,0:T(8,128)S(1)}, f32[8,8]{1,0:T(8,128)S(1)}, u32[]{:S(2)}, u32[]{:S(2)}) %collective-permute-start.13) | collective-permute-done | bytes 288 | tf_op jit(solution)/shard_map/ppermute | solution.py:19
  50.1 0.5 %collective-permute-done.11 = f32[8,8]{1,0:T(8,128)S(1)} collective-permute-done((f32[8,8]{1,0:T(8,128)S(1)}, f32[8,8]{1,0:T(8,128)S(1)}, u32[]{:S(2)}, u32[]{:S(2)}) %collective-permute-start.11) | collective-permute-done | bytes 288 | tf_op jit(solution)/shard_map/ppermute | solution.py:19
  50.7 0.1 copy.12
  50.7 0.7 %fusion.12 = f32[8,8]{1,0:T(8,128)} fusion(f32[8,8]{1,0:T(8,128)S(1)} %add_add_fusion, f32[8,8]{0,1:T(8,128)S(1)} %copy.12, f32[8]{0:T(128)S(1)} %copy-done.6), kind=kLoop, calls=%fused_computation.26 | loop fusion | flops 320 | bytes 800 | tf_op jit(solution)/shard_map/add | solution.py:176
  (22 shorter events, 0.1 us)
Async XLA Ops:
  0.6 50.1 %copy-start.6 = (f32[8]{0:T(128)S(1)}, f32[8]{0:T(128)}, u32[]{:S(2)}) copy-start(f32[8]{0:T(128)} %param.11) | copy-start | bytes 100
  2.4 26.3 %copy-start = (bf16[16,2745]{1,0:T(8,128)(2,1)}, bf16[16,2745]{1,0:T(8,128)(2,1)S(1)}, u32[]{:S(2)}) copy-start(bf16[16,2745]{1,0:T(8,128)(2,1)S(1)} %pad_maximum_fusion.1.refs_5_) | copy-start | bytes 263524
  2.4 21.4 %collective-permute-start.4 = (bf16[16,2745]{1,0:T(8,128)(2,1)S(1)}, bf16[16,2745]{1,0:T(8,128)(2,1)S(1)}, u32[]{:S(2)}, u32[]{:S(2)}) collective-permute-start(bf16[16,2745]{1,0:T(8,128)(2,1)S(1)} %pad_maximum_fusion.1.refs_5_), channel_id=1, source_target_pairs={{0,2},{2,4},{4,6},{6,0},{1,3},{3,5},{5,7},{7,1},{8,10},{10,12},{12... | collective-permute-start | bytes 263528 | tf_op jit(solution)/shard_map/ppermute | solution.py:15
  5.4 18.3 %collective-permute-start.5 = (bf16[16,2745]{1,0:T(8,128)(2,1)S(1)}, bf16[16,2745]{1,0:T(8,128)(2,1)S(1)}, u32[]{:S(2)}, u32[]{:S(2)}) collective-permute-start(bf16[16,2745]{1,0:T(8,128)(2,1)S(1)} %pad_maximum_fusion.1.refs_5_), channel_id=1, source_target_pairs={{0,4},{2,6},{4,0},{6,2},{1,5},{3,7},{5,1},{7,3},{8,12},{10,14},{12... | collective-permute-start | bytes 263528 | tf_op jit(solution)/shard_map/ppermute | solution.py:15
  14.8 7.6 %collective-permute-start = (bf16[2,16,640]{2,1,0:T(8,128)(2,1)S(1)}, bf16[2,16,640]{2,1,0:T(8,128)(2,1)S(1)}, u32[]{:S(2)}, u32[]{:S(2)}) collective-permute-start(bf16[2,16,640]{2,1,0:T(8,128)(2,1)S(1)} %get-tuple-element.5), channel_id=1, source_target_pairs={{0,2},{2,4},{4,6},{6,0},{1,3},{3,5},{5,7},{7,1},{8,10},{10,12},{12... | collective-permute-start | bytes 122888 | tf_op jit(solution)/shard_map/ppermute | solution.py:15
  14.9 8.1 %collective-permute-start.1 = (bf16[2,16,640]{2,1,0:T(8,128)(2,1)S(1)}, bf16[2,16,640]{2,1,0:T(8,128)(2,1)S(1)}, u32[]{:S(2)}, u32[]{:S(2)}) collective-permute-start(bf16[2,16,640]{2,1,0:T(8,128)(2,1)S(1)} %get-tuple-element.4), channel_id=1, source_target_pairs={{0,4},{2,6},{4,0},{6,2},{1,5},{3,7},{5,1},{7,3},{8,12},{10,14},{12... | collective-permute-start | bytes 122888 | tf_op jit(solution)/shard_map/ppermute | solution.py:15
  16.7 6.3 %collective-permute-start.2 = (bf16[2,16,640]{2,1,0:T(8,128)(2,1)S(1)}, bf16[2,16,640]{2,1,0:T(8,128)(2,1)S(1)}, u32[]{:S(2)}, u32[]{:S(2)}) collective-permute-start(bf16[2,16,640]{2,1,0:T(8,128)(2,1)S(1)} %get-tuple-element.3), channel_id=1, source_target_pairs={{0,6},{2,0},{4,2},{6,4},{1,7},{3,1},{5,3},{7,5},{8,14},{10,8},{12,... | collective-permute-start | bytes 122888 | tf_op jit(solution)/shard_map/ppermute | solution.py:15
  22.4 4.5 %collective-permute-start.6 = (bf16[16,2745]{1,0:T(8,128)(2,1)S(1)}, bf16[16,2745]{1,0:T(8,128)(2,1)S(1)}, u32[]{:S(2)}, u32[]{:S(2)}) collective-permute-start(bf16[16,2745]{1,0:T(8,128)(2,1)S(1)} %pad_maximum_fusion.1.refs_5_), channel_id=1, source_target_pairs={{0,6},{2,0},{4,2},{6,4},{1,7},{3,1},{5,3},{7,5},{8,14},{10,8},{12,... | collective-permute-start | bytes 263528 | tf_op jit(solution)/shard_map/ppermute | solution.py:15
  23.0 5.2 %collective-permute-start.3 = (bf16[64,640]{1,0:T(8,128)(2,1)S(1)}, bf16[64,640]{1,0:T(8,128)(2,1)S(1)}, u32[]{:S(2)}, u32[]{:S(2)}) collective-permute-start(bf16[64,640]{1,0:T(8,128)(2,1)S(1)} %bitcast.37), channel_id=1, source_target_pairs={{0,1},{1,0},{2,3},{3,2},{4,5},{5,4},{6,7},{7,6},{8,9},{9,8},{10,11... | collective-permute-start | bytes 245768 | tf_op jit(solution)/shard_map/ppermute | solution.py:15
  23.7 5.0 %copy-start.2 = (bf16[16,2745]{1,0:T(8,128)(2,1)}, bf16[16,2745]{1,0:T(8,128)(2,1)S(1)}, u32[]{:S(2)}) copy-start(bf16[16,2745]{1,0:T(8,128)(2,1)S(1)} %collective-permute-done.4.refs_6_) | copy-start | bytes 263524
  23.7 5.0 %copy-start.3 = (bf16[16,2745]{1,0:T(8,128)(2,1)}, bf16[16,2745]{1,0:T(8,128)(2,1)S(1)}, u32[]{:S(2)}) copy-start(bf16[16,2745]{1,0:T(8,128)(2,1)S(1)} %collective-permute-done.5.refs_7_) | copy-start | bytes 263524
  26.9 1.8 %copy-start.4 = (bf16[16,2745]{1,0:T(8,128)(2,1)}, bf16[16,2745]{1,0:T(8,128)(2,1)S(1)}, u32[]{:S(2)}) copy-start(bf16[16,2745]{1,0:T(8,128)(2,1)S(1)} %collective-permute-done.6.refs_8_) | copy-start | bytes 263524
  26.9 1.7 %collective-permute-start.7 = (bf16[64,2745]{1,0:T(8,128)(2,1)S(1)}, bf16[64,2745]{1,0:T(8,128)(2,1)S(1)}, u32[]{:S(2)}, u32[]{:S(2)}) collective-permute-start(bf16[64,2745]{1,0:T(8,128)(2,1)S(1)} %pad_maximum_fusion), channel_id=1, source_target_pairs={{0,1},{1,0},{2,3},{3,2},{4,5},{5,4},{6,7},{7,6},{8,9},{9,8},{10,11... | collective-permute-start | bytes 1054088 | tf_op jit(solution)/shard_map/ppermute | solution.py:15
  28.2 0.6 %copy-start.5 = (bf16[64,640]{1,0:T(8,128)(2,1)}, bf16[64,640]{1,0:T(8,128)(2,1)S(1)}, u32[]{:S(2)}) copy-start(bf16[64,640]{1,0:T(8,128)(2,1)S(1)} %collective-permute-done.3.refs_4_) | copy-start | bytes 245764
  28.7 0.8 %copy-start.1 = (bf16[64,2745]{1,0:T(8,128)(2,1)}, bf16[64,2745]{1,0:T(8,128)(2,1)S(1)}, u32[]{:S(2)}) copy-start(bf16[64,2745]{1,0:T(8,128)(2,1)S(1)} %collective-permute-done.7.refs_9_) | copy-start | bytes 1054084
  34.5 1.2 %collective-permute-start.8 = (f32[40]{0:T(128)S(1)}, f32[40]{0:T(128)S(1)}, u32[]{:S(2)}, u32[]{:S(2)}) collective-permute-start(f32[40]{0:T(128)S(1)} %reduce_sum.9), channel_id=1, source_target_pairs={{0,1},{1,0},{2,3},{3,2},{4,5},{5,4},{6,7},{7,6},{8,9},{9,8},{10,11... | collective-permute-start | bytes 488 | tf_op jit(solution)/shard_map/ppermute | solution.py:19
  35.8 3.6 %collective-permute-start.9 = (f32[40]{0:T(128)S(1)}, f32[40]{0:T(128)S(1)}, u32[]{:S(2)}, u32[]{:S(2)}) collective-permute-start(f32[40]{0:T(128)S(1)} %add.28), channel_id=1, source_target_pairs={{0,2},{2,0},{4,6},{6,4},{1,3},{3,1},{5,7},{7,5},{8,10},{10,8},{12,... | collective-permute-start | bytes 488 | tf_op jit(solution)/shard_map/ppermute | solution.py:19
  39.3 4.5 %collective-permute-start.10 = (f32[40]{0:T(128)S(1)}, f32[40]{0:T(128)S(1)}, u32[]{:S(2)}, u32[]{:S(2)}) collective-permute-start(f32[40]{0:T(128)S(1)} %add.29), channel_id=1, source_target_pairs={{0,4},{2,6},{4,0},{6,2},{1,5},{3,7},{5,1},{7,3},{8,12},{10,14},{12... | collective-permute-start | bytes 488 | tf_op jit(solution)/shard_map/ppermute | solution.py:19
  43.8 7.6 %copy-start.7 = (f32[40]{0:T(128)}, f32[40]{0:T(128)S(1)}, u32[]{:S(2)}) copy-start(f32[40]{0:T(128)S(1)} %add.30) | copy-start | bytes 484
  44.1 3.6 %collective-permute-start.12 = (f32[8,8]{1,0:T(8,128)S(1)}, f32[8,8]{1,0:T(8,128)S(1)}, u32[]{:S(2)}, u32[]{:S(2)}) collective-permute-start(f32[8,8]{1,0:T(8,128)S(1)} %fusion), channel_id=1, source_target_pairs={{0,16},{8,24},{16,0},{24,8},{1,17},{9,25},{17,1},{25,9},{2,18},{10... | collective-permute-start | bytes 776 | tf_op jit(solution)/shard_map/ppermute | solution.py:19
  45.6 4.5 %collective-permute-start.13 = (f32[8,8]{1,0:T(8,128)S(1)}, f32[8,8]{1,0:T(8,128)S(1)}, u32[]{:S(2)}, u32[]{:S(2)}) collective-permute-start(f32[8,8]{1,0:T(8,128)S(1)} %fusion), channel_id=1, source_target_pairs={{0,24},{8,16},{16,8},{24,0},{1,25},{9,17},{17,9},{25,1},{2,26},{10... | collective-permute-start | bytes 776 | tf_op jit(solution)/shard_map/ppermute | solution.py:19
  47.0 3.6 %collective-permute-start.11 = (f32[8,8]{1,0:T(8,128)S(1)}, f32[8,8]{1,0:T(8,128)S(1)}, u32[]{:S(2)}, u32[]{:S(2)}) collective-permute-start(f32[8,8]{1,0:T(8,128)S(1)} %fusion), channel_id=1, source_target_pairs={{0,8},{8,0},{16,24},{24,16},{1,9},{9,1},{17,25},{25,17},{2,10},{10... | collective-permute-start | bytes 776 | tf_op jit(solution)/shard_map/ppermute | solution.py:19
